TPU v7x, 32 devices: a whole 2x2x4 slice. The times are simulated.
32 devices in a mesh: gz: 2 (over x), row: 4 (over y, core), col: 4 (over z).
Axes of the slice: x: 2, y: 2, z: 4, core: 2. Of those that a mesh axis runs over, the one named last changes fastest.
Arguments:
- sections: bfloat16 [4, 2048, 2048], P('gz', 'row', 'col'), may hold values from -6 to 6
- priors: int32 [2, 4, 8, 8], P(None, 'gz', 'row', 'col'), may hold values from -64 to 64
- row_order: int32 [8], replicated, may hold values from 0 to 7, each once
Outputs:
- mesh_flows: float32 [8, 64], P('row')
Inputs may be any that keep to these rules, and one draw needn't show every extreme that they name: A permutation of the patch rows: mesh row m holds patch row row_order[m].
All inputs are finite; a program needn't handle non-finite values.
Results may differ from a plain program's by a relative error of at most 0.0003.
Values may be sent and summed in bfloat16 or wider, within the bound.
A program may use at most 64 MiB of HBM per device.

v0:
```python
import math

import jax
import jax.numpy as jnp
from jax import lax
from jax.sharding import PartitionSpec as P

PATCH = 512
STRIDE = 256
LAGS = 128
HALO = 256


def with_halo(shard, sides, width):
    for axis, dim in sides:
        devices, length = (lax.axis_size(axis), shard.shape[dim])
        up = [(i, (i + 1) % devices) for i in range(devices - 1)]
        down = [(j, i) for i, j in up]
        last = lax.slice_in_dim(shard, length - width, length, axis=dim)
        first = lax.slice_in_dim(shard, 0, width, axis=dim)
        before = lax.ppermute(last, axis, up)
        after = lax.ppermute(first, axis, down)
        shard = jnp.concatenate([before, shard, after], axis=dim)
    return shard


def shifted(value, axis, steps):
    count = lax.axis_size(axis)
    pairs = [(source, (source + steps) % count) for source in range(count)]
    return lax.ppermute(value, axis, pairs)


def dft_tables(length):
    frequencies = jnp.arange(length, dtype=jnp.int32)
    angles = jnp.mod(frequencies[:, None] * frequencies[None, :], length).astype(jnp.float32) * (
        2.0 * math.pi / length
    )
    cosine = jnp.cos(angles)
    sine_part = jnp.sin(angles)
    minus_table = jnp.concatenate([cosine, -sine_part], axis=1).astype(jnp.bfloat16)
    plus_table = jnp.concatenate([cosine, sine_part], axis=1).astype(jnp.bfloat16)
    return (minus_table, plus_table)


def spectra_of(patches, minus_table, plus_table):
    length = patches.shape[-1]
    row_pass = jnp.einsum(
        "nxy,yk->nxk", patches, minus_table, preferred_element_type=jnp.float32
    ).astype(jnp.bfloat16)
    real_rows = row_pass[:, :, :length]
    imag_rows = row_pass[:, :, length:]
    upper_stack = jnp.concatenate([real_rows, imag_rows], axis=1)
    lower_stack = jnp.concatenate([imag_rows, real_rows], axis=1)
    spec_real = (
        jnp.einsum("kx,nxm->nkm", plus_table, upper_stack, preferred_element_type=jnp.float32)
        / length
    )
    spec_imag = (
        jnp.einsum("kx,nxm->nkm", minus_table, lower_stack, preferred_element_type=jnp.float32)
        / length
    )
    return jnp.stack([spec_real, spec_imag], axis=1).astype(jnp.bfloat16)


def lag_angles(offsets, length):
    frequencies = jnp.arange(length, dtype=jnp.int32)
    shifts = offsets[:, None] + jnp.arange(LAGS, dtype=jnp.int32)[None, :] - LAGS // 2
    angles = jnp.mod(shifts[:, :, None] * frequencies[None, None, :], length).astype(
        jnp.float32
    ) * (2.0 * math.pi / length)
    return (jnp.cos(angles), jnp.sin(angles))


def flows_of(first_spec, second_spec, offsets):
    length = first_spec.shape[-1]
    first_real = first_spec[:, 0].astype(jnp.float32)
    first_imag = first_spec[:, 1].astype(jnp.float32)
    second_real = second_spec[:, 0].astype(jnp.float32)
    second_imag = second_spec[:, 1].astype(jnp.float32)
    prod_real = (first_real * second_real + first_imag * second_imag).astype(jnp.bfloat16)
    prod_imag = (first_real * second_imag - first_imag * second_real).astype(jnp.bfloat16)
    row_cosine, row_sine = lag_angles(offsets[0], length)
    column_cosine, column_sine = lag_angles(offsets[1], length)
    products = jnp.concatenate([prod_real, prod_imag], axis=2)
    column_real = jnp.concatenate([column_cosine, -column_sine], axis=2).astype(jnp.bfloat16)
    column_imag = jnp.concatenate([column_sine, column_cosine], axis=2).astype(jnp.bfloat16)
    half_real = jnp.einsum(
        "nkl,nul->nku", products, column_real, preferred_element_type=jnp.float32
    ).astype(jnp.bfloat16)
    half_imag = jnp.einsum(
        "nkl,nul->nku", products, column_imag, preferred_element_type=jnp.float32
    ).astype(jnp.bfloat16)
    row_table = jnp.concatenate([row_cosine, -row_sine], axis=2).astype(jnp.bfloat16)
    stacked = jnp.concatenate([half_real, half_imag], axis=1)
    surface = (
        jnp.einsum("ntk,nku->ntu", row_table, stacked, preferred_element_type=jnp.float32) / length
    )
    weights = surface * surface
    displacement = (jnp.arange(LAGS, dtype=jnp.int32) - LAGS // 2).astype(jnp.float32)
    weight_sum = 1.0 + jnp.sum(weights, axis=(1, 2))
    row_shift = jnp.sum(weights * displacement[None, :, None], axis=(1, 2)) / weight_sum
    column_shift = jnp.sum(weights * displacement[None, None, :], axis=(1, 2)) / weight_sum
    return jnp.stack(
        [offsets[0].astype(jnp.float32) + row_shift, offsets[1].astype(jnp.float32) + column_shift],
        axis=0,
    )


def body(sections, priors, row_order):
    sec_count = sections.shape[0]
    block_side = sections.shape[1]
    per_side = block_side // STRIDE
    place_count = per_side * per_side
    margin = HALO // 2
    minus_table, plus_table = dft_tables(PATCH)
    offsets_all = jnp.transpose(priors, (2, 3, 0, 1)).reshape(place_count, 2, sec_count)
    positions = jnp.arange(place_count, dtype=jnp.int32)

    def cut_window(extended, position):
        top_edge = position // per_side * STRIDE
        left_edge = position % per_side * STRIDE
        return lax.dynamic_slice(
            extended, (jnp.int32(0), top_edge, left_edge), (extended.shape[0], PATCH, PATCH)
        )

    arrived = shifted(sections[:1], "gz", -1)
    extended = with_halo(
        jnp.concatenate([sections, arrived], axis=0), (("row", 1), ("col", 2)), margin
    )

    def place_flows(inputs):
        position, offsets = inputs
        section_spectra = spectra_of(cut_window(extended, position), minus_table, plus_table)
        return flows_of(section_spectra[:-1], section_spectra[1:], offsets)

    all_flows = lax.map(place_flows, (positions, offsets_all))
    local_table = jnp.transpose(all_flows.reshape(per_side, per_side, 2, sec_count), (2, 3, 0, 1))
    flat_flows = local_table.reshape(1, 2 * sec_count * place_count)
    gathered = lax.all_gather(flat_flows, ("gz", "row", "col"), axis=0, tiled=True)
    size_gz = lax.axis_size("gz")
    size_row = lax.axis_size("row")
    size_col = lax.axis_size("col")
    whole_grid = gathered.reshape(size_gz, size_row, size_col, 2, sec_count, per_side, per_side)
    whole_grid = jnp.transpose(whole_grid, (3, 0, 4, 1, 5, 2, 6)).reshape(
        2, size_gz * sec_count, size_row * per_side, size_col * per_side
    )
    rows_each = row_order.shape[0] // size_row
    owned = lax.dynamic_slice_in_dim(row_order, lax.axis_index("row") * rows_each, rows_each)
    selector = (owned[:, None] == jnp.arange(row_order.shape[0], dtype=jnp.int32)[None, :]).astype(
        jnp.float32
    )
    picked = jnp.einsum("jr,csrk->jcsk", selector, whole_grid, precision=lax.Precision.HIGHEST)
    return picked.reshape(rows_each, 2 * size_gz * sec_count * size_col * per_side)


def solution(mesh):
    placed = (P("gz", "row", "col"), P(None, "gz", "row", "col"), P())
    return jax.shard_map(
        body, mesh=mesh, in_specs=placed, out_specs=P("row", None), check_vma=False
    )
```

profile of v0, /device:TPU:0, one launch (start us, length us, event | category | flops | bytes accessed | tf_op | source)
XLA Modules:
  0.0 189.6 jit_solution(16648246001251315316)
XLA Ops:
  0.0 1.1 slice.97
  1.1 3.0 %collective-permute-start = (bf16[1,512,512]{2,1,0:T(8,128)(2,1)S(1)}, bf16[1,512,512]{2,1,0:T(8,128)(2,1)S(1)}, u32[]{:S(2)}, u32[]{:S(2)}) collective-permute-start(bf16[1,512,512]{2,1,0:T(8,128)(2,1)S(1)} %slice.97), channel_id=1, source_target_pairs={{0,16},{16,0},{1,17},{17,1},{2,18},{18,2},{3,19},{19,3},{4,20},{20... | collective-permute-start | bytes 1572872 | tf_op jit(solution)/shard_map/ppermute | solution.py:30
  4.1 1.3 constant_dynamic-update-slice_fusion.1
  5.4 10.6 %collective-permute-done = bf16[1,512,512]{2,1,0:T(8,128)(2,1)S(1)} collective-permute-done((bf16[1,512,512]{2,1,0:T(8,128)(2,1)S(1)}, bf16[1,512,512]{2,1,0:T(8,128)(2,1)S(1)}, u32[]{:S(2)}, u32[]{:S(2)}) %collective-permute-start) | collective-permute-done | bytes 524320 | tf_op jit(solution)/shard_map/ppermute | solution.py:30
  16.2 1.3 collective-permute-start.1
  17.5 1.3 collective-permute-start.2
  18.8 4.3 %collective-permute-done.2 = bf16[3,128,512]{2,1,0:T(8,128)(2,1)S(1)} collective-permute-done((bf16[3,128,512]{2,1,0:T(8,128)(2,1)S(1)}, bf16[3,128,512]{2,1,0:T(8,128)(2,1)S(1)}, u32[]{:S(2)}, u32[]{:S(2)}) %collective-permute-start.2) | collective-permute-done | bytes 393248 | tf_op jit(solution)/shard_map/ppermute | solution.py:22
  23.1 1.2 pad_maximum_fusion.12
  24.3 4.3 %collective-permute-start.3 = (bf16[3,768,128]{2,1,0:T(8,128)(2,1)}, bf16[3,768,128]{2,1,0:T(8,128)(2,1)}, u32[]{:S(2)}, u32[]{:S(2)}) collective-permute-start(bf16[3,768,128]{2,1,0:T(8,128)(2,1)} %get-tuple-element.187), channel_id=1, source_target_pairs={{0,1},{1,2},{2,3},{4,5},{5,6},{6,7},{8,9},{9,10},{10,11},{12,13},{... | collective-permute-start | bytes 1769480 | tf_op jit(solution)/shard_map/ppermute | solution.py:21
  28.7 1.3 collective-permute-start.4
  30.2 4.0 %fusion.71 = bf16[512,512]{1,0:T(8,128)(2,1)S(1)} fusion(), kind=kLoop, calls=%fused_computation.104 | loop fusion | flops 3932160 | bytes 524288 | tf_op jit(solution)/shard_map/convert.13
  34.1 4.3 %negate_convert_fusion.2 = (bf16[512,512]{1,0:T(8,128)(2,1)S(1)}, bf16[512,512]{1,0:T(8,128)(2,1)S(1)}) fusion(), kind=kLoop, calls=%fused_computation.95 | loop fusion | flops 4456448 | bytes 1048576 | tf_op jit(solution)/shard_map/convert.15
  38.5 1.3 pad_maximum_fusion.8
  39.7 2.6 %collective-permute-done.4 = bf16[3,768,128]{2,1,0:T(8,128)(2,1)} collective-permute-done((bf16[3,768,128]{2,1,0:T(8,128)(2,1)}, bf16[3,768,128]{2,1,0:T(8,128)(2,1)}, u32[]{:S(2)}, u32[]{:S(2)}) %collective-permute-start.4) | collective-permute-done | bytes 589856 | tf_op jit(solution)/shard_map/ppermute | solution.py:22
  42.3 4.3 %pad_maximum_fusion.7 = bf16[3,768,768]{2,1,0:T(8,128)(2,1)} fusion(bf16[3,768,128]{2,1,0:T(8,128)(2,1)} %collective-permute-done.4, bf16[3,128,512]{2,1,0:T(8,128)(2,1)S(1)} %collective-permute-done.2, bf16[3,512,512]{2,1,0:T(8,128)(2,1)S(1)} %constant_dynamic-update-slice_fusion, bf16[3,128,512]{2,1,0:T(8,128)(2,1)S(1)} %collective-permute-done.1, ...), kind=kLoop, calls=%fused_computation.86 | loop fusion | flops 17694720 | bytes 7077888 | tf_op jit(solution)/shard_map/concatenate | solution.py:23
  46.7 75.7 %while.13 = (s32[]{:T(128)}, f32[4,2,2]{2,1,0:T(2,128)S(1)}, s32[4,2,2]{2,1,0:T(2,128)S(1)}, s32[4]{0:T(128)S(1)}, bf16[3,768,768]{2,1,0:T(8,128)(2,1)}, /*index...) while((s32[]{:T(128)}, f32[4,2,2]{2,1,0:T(2,128)S(1)}, ...), condition=%wide.region_4.5_spmd, body=%wide.region_0.4_spmd.sunk | while | flops 5477073920 | bytes 42212972 | solution.py:136
  46.7 0.6 dynamic_slice.35
  49.8 3.5 %convolution_convert_fusion.2 = bf16[3,512,1024]{2,1,0:T(8,128)(2,1)S(1)} fusion(bf16[3,768,768]{2,1,0:T(8,128)(2,1)} %get-tuple-element.304, s32[]{:T(128)S(6)} %select_n.116, s32[]{:T(128)S(6)} %select_n.118, bf16[512,1024]{1,0:T(8,128)(2,1)} %get-tuple-element.305), kind=kOutput, calls=%fused_computation.14.clone.1 | convolution fusion | flops 1612185600 | bytes 5767176 | tf_op jit(solution)/shard_map/while/body/eval_jaxpr/nxy,yk->nxk/dot_general | solution.py:47
  53.3 0.3 fusion.102
  53.6 1.9 fusion.104
  55.5 1.9 fusion.103
  57.4 0.8 fusion.105
  58.3 2.5 %negate_convert_fusion.4 = (bf16[2,128,512]{2,1,0:T(8,128)(2,1)S(1)}, bf16[2,128,512]{2,1,0:T(8,128)(2,1)S(1)}, bf16[2,128,512]{2,1,0:T(8,128)(2,1)S(1)}) fusion(s32[2,128]{1,0:T(2,128)S(1)} %get-tuple-element.262), kind=kLoop, calls=%fused_computation.56.clone.1 | loop fusion | flops 2359296 | bytes 787456 | tf_op jit(solution)/shard_map/convert.3
  60.8 0.9 fusion.107
  61.7 0.9 fusion.106
  62.7 2.5 %cosine_convert_fusion.4 = (bf16[2,128,512]{2,1,0:T(8,128)(2,1)S(1)}, bf16[2,128,512]{2,1,0:T(8,128)(2,1)S(1)}) fusion(s32[2,128]{1,0:T(2,128)S(1)} %get-tuple-element.266), kind=kLoop, calls=%fused_computation.61.clone.1 | loop fusion | flops 2228224 | bytes 525312 | tf_op jit(solution)/shard_map/convert.10
  65.2 0.4 multiply_reduce_fusion.3
  65.6 0.6 dynamic_slice.35
  68.7 3.5 %convolution_convert_fusion.2 = bf16[3,512,1024]{2,1,0:T(8,128)(2,1)S(1)} fusion(bf16[3,768,768]{2,1,0:T(8,128)(2,1)} %get-tuple-element.304, s32[]{:T(128)S(6)} %select_n.116, s32[]{:T(128)S(6)} %select_n.118, bf16[512,1024]{1,0:T(8,128)(2,1)} %get-tuple-element.305), kind=kOutput, calls=%fused_computation.14.clone.1 | convolution fusion | flops 1612185600 | bytes 5767176 | tf_op jit(solution)/shard_map/while/body/eval_jaxpr/nxy,yk->nxk/dot_general | solution.py:47
  72.3 0.3 fusion.102
  72.6 1.9 fusion.104
  74.5 1.9 fusion.103
  76.4 0.8 fusion.105
  77.2 2.5 %negate_convert_fusion.4 = (bf16[2,128,512]{2,1,0:T(8,128)(2,1)S(1)}, bf16[2,128,512]{2,1,0:T(8,128)(2,1)S(1)}, bf16[2,128,512]{2,1,0:T(8,128)(2,1)S(1)}) fusion(s32[2,128]{1,0:T(2,128)S(1)} %get-tuple-element.262), kind=kLoop, calls=%fused_computation.56.clone.1 | loop fusion | flops 2359296 | bytes 787456 | tf_op jit(solution)/shard_map/convert.3
  79.7 0.9 fusion.107
  80.6 0.9 fusion.106
  81.6 2.5 %cosine_convert_fusion.4 = (bf16[2,128,512]{2,1,0:T(8,128)(2,1)S(1)}, bf16[2,128,512]{2,1,0:T(8,128)(2,1)S(1)}) fusion(s32[2,128]{1,0:T(2,128)S(1)} %get-tuple-element.266), kind=kLoop, calls=%fused_computation.61.clone.1 | loop fusion | flops 2228224 | bytes 525312 | tf_op jit(solution)/shard_map/convert.10
  84.1 0.4 multiply_reduce_fusion.3
  84.5 0.6 dynamic_slice.35
  87.7 3.5 %convolution_convert_fusion.2 = bf16[3,512,1024]{2,1,0:T(8,128)(2,1)S(1)} fusion(bf16[3,768,768]{2,1,0:T(8,128)(2,1)} %get-tuple-element.304, s32[]{:T(128)S(6)} %select_n.116, s32[]{:T(128)S(6)} %select_n.118, bf16[512,1024]{1,0:T(8,128)(2,1)} %get-tuple-element.305), kind=kOutput, calls=%fused_computation.14.clone.1 | convolution fusion | flops 1612185600 | bytes 5767176 | tf_op jit(solution)/shard_map/while/body/eval_jaxpr/nxy,yk->nxk/dot_general | solution.py:47
  91.2 0.3 fusion.102
  91.5 1.9 fusion.104
  93.4 1.9 fusion.103
  95.3 0.8 fusion.105
  96.2 2.5 %negate_convert_fusion.4 = (bf16[2,128,512]{2,1,0:T(8,128)(2,1)S(1)}, bf16[2,128,512]{2,1,0:T(8,128)(2,1)S(1)}, bf16[2,128,512]{2,1,0:T(8,128)(2,1)S(1)}) fusion(s32[2,128]{1,0:T(2,128)S(1)} %get-tuple-element.262), kind=kLoop, calls=%fused_computation.56.clone.1 | loop fusion | flops 2359296 | bytes 787456 | tf_op jit(solution)/shard_map/convert.3
  98.6 0.9 fusion.107
  99.6 0.9 fusion.106
  100.5 2.5 %cosine_convert_fusion.4 = (bf16[2,128,512]{2,1,0:T(8,128)(2,1)S(1)}, bf16[2,128,512]{2,1,0:T(8,128)(2,1)S(1)}) fusion(s32[2,128]{1,0:T(2,128)S(1)} %get-tuple-element.266), kind=kLoop, calls=%fused_computation.61.clone.1 | loop fusion | flops 2228224 | bytes 525312 | tf_op jit(solution)/shard_map/convert.10
  103.0 0.4 multiply_reduce_fusion.3
  103.5 0.6 dynamic_slice.35
  106.6 3.5 %convolution_convert_fusion.2 = bf16[3,512,1024]{2,1,0:T(8,128)(2,1)S(1)} fusion(bf16[3,768,768]{2,1,0:T(8,128)(2,1)} %get-tuple-element.304, s32[]{:T(128)S(6)} %select_n.116, s32[]{:T(128)S(6)} %select_n.118, bf16[512,1024]{1,0:T(8,128)(2,1)} %get-tuple-element.305), kind=kOutput, calls=%fused_computation.14.clone.1 | convolution fusion | flops 1612185600 | bytes 5767176 | tf_op jit(solution)/shard_map/while/body/eval_jaxpr/nxy,yk->nxk/dot_general | solution.py:47
  110.1 0.3 fusion.102
  110.4 1.9 fusion.104
  112.3 1.9 fusion.103
  114.2 0.8 fusion.105
  115.1 2.5 %negate_convert_fusion.4 = (bf16[2,128,512]{2,1,0:T(8,128)(2,1)S(1)}, bf16[2,128,512]{2,1,0:T(8,128)(2,1)S(1)}, bf16[2,128,512]{2,1,0:T(8,128)(2,1)S(1)}) fusion(s32[2,128]{1,0:T(2,128)S(1)} %get-tuple-element.262), kind=kLoop, calls=%fused_computation.56.clone.1 | loop fusion | flops 2359296 | bytes 787456 | tf_op jit(solution)/shard_map/convert.3
  117.6 0.9 fusion.107
  118.5 0.9 fusion.106
  119.5 2.5 %cosine_convert_fusion.4 = (bf16[2,128,512]{2,1,0:T(8,128)(2,1)S(1)}, bf16[2,128,512]{2,1,0:T(8,128)(2,1)S(1)}) fusion(s32[2,128]{1,0:T(2,128)S(1)} %get-tuple-element.266), kind=kLoop, calls=%fused_computation.61.clone.1 | loop fusion | flops 2228224 | bytes 525312 | tf_op jit(solution)/shard_map/convert.10
  122.0 0.4 multiply_reduce_fusion.3
  122.6 65.3 %all-gather = f32[32,1,16]{2,1,0:T(1,128)S(1)} all-gather(f32[1,1,16]{2,1,0:T(1,128)S(1)} %reshape.208), channel_id=1, replica_groups=mesh['gz'=2,'row'=4,'col'=4] {'gz','row','col'}, dimensions={0}, use_global_device_ids=true | all-gather | bytes 2112 | tf_op jit(solution)/shard_map/all_gather | solution.py:139
  188.1 0.5 copy.22
  188.6 0.1 reshape.193
  188.8 0.8 fusion.72
  (50 shorter events, 1.3 us)
Async XLA Ops:
  1.1 15.0 %collective-permute-start = (bf16[1,512,512]{2,1,0:T(8,128)(2,1)S(1)}, bf16[1,512,512]{2,1,0:T(8,128)(2,1)S(1)}, u32[]{:S(2)}, u32[]{:S(2)}) collective-permute-start(bf16[1,512,512]{2,1,0:T(8,128)(2,1)S(1)} %slice.97), channel_id=1, source_target_pairs={{0,16},{16,0},{1,17},{17,1},{2,18},{18,2},{3,19},{19,3},{4,20},{20... | collective-permute-start | bytes 1572872 | tf_op jit(solution)/shard_map/ppermute | solution.py:30
  16.1 13.8 %copy-start.1 = (s32[2,2,2,2]{3,2,1,0:T(2,128)S(1)}, s32[2,2,2,2]{3,2,1,0:T(2,128)}, u32[]{:S(2)}) copy-start(s32[2,2,2,2]{3,2,1,0:T(2,128)} %param.6) | copy-start | bytes 196
  16.1 13.9 %copy-start.2 = (s32[8]{0:T(128)S(1)}, s32[8]{0:T(128)}, u32[]{:S(2)}) copy-start(s32[8]{0:T(128)} %param.7) | copy-start | bytes 100
  16.2 2.6 %collective-permute-start.1 = (bf16[3,128,512]{2,1,0:T(8,128)(2,1)S(1)}, bf16[3,128,512]{2,1,0:T(8,128)(2,1)S(1)}, u32[]{:S(2)}, u32[]{:S(2)}) collective-permute-start(bf16[3,128,512]{2,1,0:T(8,128)(2,1)S(1)} %get-tuple-element.189), channel_id=1, source_target_pairs={{0,4},{4,8},{8,12},{1,5},{5,9},{9,13},{2,6},{6,10},{10,14},{3,7},{... | collective-permute-start | bytes 1179656 | tf_op jit(solution)/shard_map/ppermute | solution.py:21
  17.5 5.6 %collective-permute-start.2 = (bf16[3,128,512]{2,1,0:T(8,128)(2,1)S(1)}, bf16[3,128,512]{2,1,0:T(8,128)(2,1)S(1)}, u32[]{:S(2)}, u32[]{:S(2)}) collective-permute-start(bf16[3,128,512]{2,1,0:T(8,128)(2,1)S(1)} %get-tuple-element.190), channel_id=1, source_target_pairs={{4,0},{8,4},{12,8},{5,1},{9,5},{13,9},{6,2},{10,6},{14,10},{7,3},{... | collective-permute-start | bytes 1179656 | tf_op jit(solution)/shard_map/ppermute | solution.py:22
  24.3 15.4 %collective-permute-start.3 = (bf16[3,768,128]{2,1,0:T(8,128)(2,1)}, bf16[3,768,128]{2,1,0:T(8,128)(2,1)}, u32[]{:S(2)}, u32[]{:S(2)}) collective-permute-start(bf16[3,768,128]{2,1,0:T(8,128)(2,1)} %get-tuple-element.187), channel_id=1, source_target_pairs={{0,1},{1,2},{2,3},{4,5},{5,6},{6,7},{8,9},{9,10},{10,11},{12,13},{... | collective-permute-start | bytes 1769480 | tf_op jit(solution)/shard_map/ppermute | solution.py:21
  28.7 13.7 %collective-permute-start.4 = (bf16[3,768,128]{2,1,0:T(8,128)(2,1)}, bf16[3,768,128]{2,1,0:T(8,128)(2,1)}, u32[]{:S(2)}, u32[]{:S(2)}) collective-permute-start(bf16[3,768,128]{2,1,0:T(8,128)(2,1)} %get-tuple-element.188), channel_id=1, source_target_pairs={{1,0},{2,1},{3,2},{5,4},{6,5},{7,6},{9,8},{10,9},{11,10},{13,12},{... | collective-permute-start | bytes 1769480 | tf_op jit(solution)/shard_map/ppermute | solution.py:22
  53.6 1.9 %copy-start = (bf16[512,1024]{1,0:T(8,128)(2,1)S(1)}, bf16[512,1024]{1,0:T(8,128)(2,1)}, u32[]{:S(2)}) copy-start(bf16[512,1024]{1,0:T(8,128)(2,1)} %get-tuple-element.305) | copy-start | bytes 3145732 | tf_op jit(solution)/shard_map/while
  72.6 1.9 %copy-start = (bf16[512,1024]{1,0:T(8,128)(2,1)S(1)}, bf16[512,1024]{1,0:T(8,128)(2,1)}, u32[]{:S(2)}) copy-start(bf16[512,1024]{1,0:T(8,128)(2,1)} %get-tuple-element.305) | copy-start | bytes 3145732 | tf_op jit(solution)/shard_map/while
  91.5 1.9 %copy-start = (bf16[512,1024]{1,0:T(8,128)(2,1)S(1)}, bf16[512,1024]{1,0:T(8,128)(2,1)}, u32[]{:S(2)}) copy-start(bf16[512,1024]{1,0:T(8,128)(2,1)} %get-tuple-element.305) | copy-start | bytes 3145732 | tf_op jit(solution)/shard_map/while
  110.4 1.9 %copy-start = (bf16[512,1024]{1,0:T(8,128)(2,1)S(1)}, bf16[512,1024]{1,0:T(8,128)(2,1)}, u32[]{:S(2)}) copy-start(bf16[512,1024]{1,0:T(8,128)(2,1)} %get-tuple-element.305) | copy-start | bytes 3145732 | tf_op jit(solution)/shard_map/while
where the time goes:
time: 190 us
  blocking collectives  65.3 us (34%)
  matrix products  39 us (21%)
  other arithmetic  38.4 us (20%)
  waiting for transfers between devices  17.5 us (9%)
  starting transfers between devices  11.3 us (6%)
  loops' own time  10.6 us (6%)
  local copies, waits for them, and re-layouts  7.37 us (4%)
    all_gather x1, blocking collectives, body(): lax.all_gather(flat_flows, ('gz', 'row', 'col'), axis=0, tiled=True)  65.3 us
    another operation x11, other arithmetic  28 us
    dot_general x4, matrix products, spectra_of(): jnp.einsum('nxy,yk->nxk', patches, minus_table, preferred_element_type=jn...  14.1 us
    ppermute x1, waiting for transfers between devices, shifted(): return lax.ppermute(value, axis, pairs)  10.6 us
    another operation x1, loops' own time, body(): all_flows = lax.map(place_flows, (positions, offsets_all))  10.6 us
    dot_general x4, matrix products, spectra_of(): jnp.einsum('kx,nxm->nkm', minus_table, lower_stack, preferred_element_typ...  7.51 us
    dot_general x4, matrix products, spectra_of(): jnp.einsum('kx,nxm->nkm', plus_table, upper_stack, preferred_element_type...  7.51 us
    ppermute x2, waiting for transfers between devices, with_halo(): after = lax.ppermute(first, axis, down)  6.89 us
  transfers between devices with their start and end apart: 5, of which 3 were waited for; matrix products, arithmetic and copies ran while one was open for 6% of the time, Pallas kernels for 0%

commit v1 on v0

v1 whole, which is shorter than its diff:
```python
import math

import jax
import jax.numpy as jnp
import numpy as np
from jax import lax
from jax.experimental import pallas as pl
from jax.experimental.pallas import tpu as pltpu
from jax.sharding import PartitionSpec as P

PATCH = 512
STRIDE = 256
LAGS = 128
HALO = 256
HALF = PATCH // 2
QUARTER = PATCH // 4
KROWS = HALF + 16


def angle_of(products):
    return (products % PATCH) * (2.0 * math.pi / PATCH)


def dft_table():
    k = np.arange(HALF)[:, None]
    x = np.arange(PATCH)[None, :]
    table = np.zeros((2 * KROWS, PATCH))
    table[:HALF] = np.cos(angle_of(k * x))
    table[HALF] = np.cos(angle_of(HALF * x[0]))
    table[KROWS : KROWS + HALF] = -np.sin(angle_of(k * x))
    return table


def split_tables():
    y = np.arange(QUARTER)[:, None]
    blocks = []
    for g in range(4):
        l = 4 * np.arange(QUARTER)[None, :] + g
        c, s = np.cos(angle_of(y * l)), np.sin(angle_of(y * l))
        blocks.append(np.block([[c, -s], [s, c]]))
    return np.stack(blocks)


def lag_tables():
    lag = np.arange(2 * LAGS)[:, None] - LAGS
    l = np.concatenate([4 * np.arange(QUARTER) + g for g in range(4)])[None, :]
    k = np.arange(KROWS)[None, :]
    weight = np.where(k == 0, 1.0, np.where(k < HALF, 2.0, np.where(k == HALF, 1.0, 0.0)))
    col = (np.cos(angle_of(lag * l)), np.sin(angle_of(lag * l)))
    row_cos = np.cos(angle_of(lag * k)) * weight
    row_sin = -np.sin(angle_of(lag * k)) * weight
    row = np.concatenate([row_cos, row_sin], axis=1)
    return col[0], col[1], row


def bf16_const(value):
    return value.astype(np.float32).astype(jnp.bfloat16)


def f32_const(value):
    return bf16_const(value).astype(np.float32)


def spectrum_pair(ext, section, i, dft_ref, wg_ref, spec_ref, pq_ref, base):
    window = ext[section, pl.ds(pl.multiple_of(i * STRIDE, STRIDE), PATCH), :]
    pq_ref[...] = jnp.dot(dft_ref[...], window, preferred_element_type=jnp.float32)
    for j in range(2):
        p, q = [], []
        for t in range(4):
            lanes = slice(j * STRIDE + t * QUARTER, j * STRIDE + (t + 1) * QUARTER)
            p.append(pq_ref[:KROWS, lanes])
            q.append(pq_ref[KROWS:, lanes])
        ps, pd, qs, qd = p[0] + p[2], p[0] - p[2], q[0] + q[2], q[0] - q[2]
        pt, pu, qt, qu = p[1] + p[3], p[1] - p[3], q[1] + q[3], q[1] - q[3]
        groups = ((ps + pt, qs + qt), (pd + qu, qd - pu), (ps - pt, qs - qt), (pd - qu, qd + pu))
        for g, (real, imag) in enumerate(groups):
            left = jnp.concatenate([real.astype(jnp.bfloat16), imag.astype(jnp.bfloat16)], axis=1)
            out = jnp.dot(left, wg_ref[g], preferred_element_type=jnp.float32).astype(jnp.bfloat16)
            lo = g * QUARTER
            spec_ref[base + j, :, lo : lo + QUARTER] = out[:, :QUARTER]
            spec_ref[base + j, :, PATCH + lo : PATCH + lo + QUARTER] = out[:, QUARTER:]


def lag_rows(table, prior):
    tiles = [
        table[t, pl.ds(prior + LAGS // 2, LAGS), :].astype(jnp.bfloat16)
        for t in range(table.shape[0])
    ]
    return jnp.concatenate(tiles, axis=1)


def lane_tiles(table):
    width = -(-table.shape[1] // LAGS) * LAGS
    table = np.pad(table, ((0, 0), (0, width - table.shape[1])))
    return np.stack(np.split(table, width // LAGS, axis=1))


def pair_flow(first, second, p, q, spec_ref, colc_ref, cols_ref, row_ref):
    f32 = jnp.float32
    ar = spec_ref[first, :, :PATCH].astype(f32)
    ai = spec_ref[first, :, PATCH:].astype(f32)
    br = spec_ref[second, :, :PATCH].astype(f32)
    bi = spec_ref[second, :, PATCH:].astype(f32)
    cr = (ar * br + ai * bi).astype(jnp.bfloat16)
    ci = (ar * bi - ai * br).astype(jnp.bfloat16)
    ec = lag_rows(colc_ref, q)
    es = lag_rows(cols_ref, q)
    left = jnp.concatenate([cr, ci], axis=1)
    right = jnp.concatenate(
        [jnp.concatenate([ec, -es], axis=1), jnp.concatenate([es, ec], axis=1)], axis=0
    )
    half = lax.dot_general(
        left, right, (((1,), (1,)), ((), ())), preferred_element_type=f32
    ).astype(jnp.bfloat16)
    stacked = jnp.concatenate([half[:, :LAGS], half[:, LAGS:]], axis=0)
    rows = lag_rows(row_ref, p)[:, : 2 * KROWS]
    surface = jnp.dot(rows, stacked, preferred_element_type=f32) * (1.0 / PATCH**3)
    w = surface * surface
    da = (lax.broadcasted_iota(jnp.int32, (LAGS, LAGS), 0) - LAGS // 2).astype(f32)
    db = (lax.broadcasted_iota(jnp.int32, (1, LAGS), 1) - LAGS // 2).astype(f32)
    col_w = jnp.sum(w, axis=0, keepdims=True)
    total = 1.0 + jnp.sum(col_w, axis=1, keepdims=True)
    row_m = jnp.sum(jnp.sum(w * da, axis=0, keepdims=True), axis=1, keepdims=True)
    col_m = jnp.sum(col_w * db, axis=1, keepdims=True)
    return p.astype(f32) + row_m / total, q.astype(f32) + col_m / total


def kernel(pri_ref, ext, dft_ref, wg_ref, colc_ref, cols_ref, row_ref, out_ref, spec_ref, pq_ref):
    def spectra(n, carry):
        spectrum_pair(ext, n // 2, n % 2, dft_ref, wg_ref, spec_ref, pq_ref, n * 2)
        return carry

    lax.fori_loop(0, 6, spectra, 0)
    lane = lax.broadcasted_iota(jnp.int32, (1, LAGS), 1)

    def pairs(n, carry):
        a, b = pair_flow(
            n, n + 4, pri_ref[n], pri_ref[8 + n], spec_ref, colc_ref, cols_ref, row_ref
        )
        out_ref[pl.ds(n, 1), :] = jnp.where(lane == 0, a, b)
        return carry

    lax.fori_loop(0, 8, pairs, 0)


def with_halo(shard, sides, width):
    for axis, dim in sides:
        devices, length = (lax.axis_size(axis), shard.shape[dim])
        up = [(i, (i + 1) % devices) for i in range(devices - 1)]
        down = [(j, i) for i, j in up]
        last = lax.slice_in_dim(shard, length - width, length, axis=dim)
        first = lax.slice_in_dim(shard, 0, width, axis=dim)
        before = lax.ppermute(last, axis, up)
        after = lax.ppermute(first, axis, down)
        shard = jnp.concatenate([before, shard, after], axis=dim)
    return shard


def shifted(value, axis, steps):
    count = lax.axis_size(axis)
    pairs = [(source, (source + steps) % count) for source in range(count)]
    return lax.ppermute(value, axis, pairs)


def body(sections, priors, row_order):
    sec_count = sections.shape[0]
    per_side = sections.shape[1] // STRIDE
    place_count = per_side * per_side
    arrived = shifted(sections[:1], "gz", -1)
    extended = with_halo(
        jnp.concatenate([sections, arrived], axis=0), (("row", 1), ("col", 2)), HALO // 2
    )
    colc, cols, row = lag_tables()
    vmem = pl.BlockSpec(memory_space=pltpu.VMEM)
    flows = pl.pallas_call(
        kernel,
        out_shape=jax.ShapeDtypeStruct((8, LAGS), jnp.float32),
        in_specs=[pl.BlockSpec(memory_space=pltpu.SMEM)] + [vmem] * 6,
        out_specs=vmem,
        scratch_shapes=[
            pltpu.VMEM((12, KROWS, 2 * PATCH), jnp.bfloat16),
            pltpu.VMEM((2 * KROWS, 768), jnp.float32),
        ],
        compiler_params=pltpu.CompilerParams(vmem_limit_bytes=50 << 20),
    )(
        priors.reshape(-1),
        extended,
        bf16_const(dft_table()),
        bf16_const(split_tables()),
        f32_const(lane_tiles(colc)),
        f32_const(lane_tiles(cols)),
        f32_const(lane_tiles(row)),
    )
    flat_flows = flows[:, :2].T.reshape(1, 2 * sec_count * place_count)
    gathered = lax.all_gather(flat_flows, ("gz", "row", "col"), axis=0, tiled=True)
    size_gz = lax.axis_size("gz")
    size_row = lax.axis_size("row")
    size_col = lax.axis_size("col")
    whole_grid = gathered.reshape(size_gz, size_row, size_col, 2, sec_count, per_side, per_side)
    whole_grid = jnp.transpose(whole_grid, (3, 0, 4, 1, 5, 2, 6)).reshape(
        2, size_gz * sec_count, size_row * per_side, size_col * per_side
    )
    rows_each = row_order.shape[0] // size_row
    owned = lax.dynamic_slice_in_dim(row_order, lax.axis_index("row") * rows_each, rows_each)
    selector = (owned[:, None] == jnp.arange(row_order.shape[0], dtype=jnp.int32)[None, :]).astype(
        jnp.float32
    )
    picked = jnp.einsum("jr,csrk->jcsk", selector, whole_grid, precision=lax.Precision.HIGHEST)
    return picked.reshape(rows_each, 2 * size_gz * sec_count * size_col * per_side)


def solution(mesh):
    placed = (P("gz", "row", "col"), P(None, "gz", "row", "col"), P())
    return jax.shard_map(
        body, mesh=mesh, in_specs=placed, out_specs=P("row", None), check_vma=False
    )
```

time: 190 us -> 125 us (0.66)
  matrix products: 39 us -> 0.76 us
  other arithmetic: 38.4 us -> 4.55 us
  Pallas kernels: 0 us -> 13.6 us
  waiting for transfers between devices: 17.5 us -> 28.2 us
  loops' own time: 10.6 us -> 0 us
  local copies, waits for them, and re-layouts: 7.37 us -> 2.57 us
    dot_general x24 -> x0, matrix products: 38.3 us -> none  [the longest x4 14.1 us: spectra_of(): jnp.einsum('nxy,yk->nxk', patches, minus_table, preferred_element_type=jn...]
    another operation x11 -> x0, other arithmetic: 28 us -> none
    pallas_call x0 -> x1, Pallas kernels: none -> 13.6 us  [body(): pl.pallas_call(kernel, out_shape=jax.ShapeDtypeStruct((8, LAGS), jnp.floa...]
    another operation x1 -> x0, loops' own time: 10.6 us -> none  [body(): all_flows = lax.map(place_flows, (positions, offsets_all))]
    ppermute x2, waiting for transfers between devices: 0.01 us -> 7.48 us  [with_halo(): before = lax.ppermute(last, axis, up)]
    convert_element_type x8 -> x0, other arithmetic: 3.08 us -> none  [the longest x4 3.06 us: flows_of(): (first_real * second_real + first_imag * second_imag).astype(jnp.bfloat16)]
    dynamic_slice x8 -> x0, local copies, waits for them, and re-layouts: 2.43 us -> none  [body(): all_flows = lax.map(place_flows, (positions, offsets_all))]
    ppermute x2, waiting for transfers between devices: 6.89 us -> 8.89 us  [with_halo(): after = lax.ppermute(first, axis, down)]
  transfers between devices with their start and end apart: 5 -> 5, of which waited for: 3 -> 4; matrix products, arithmetic and copies ran while one was open for 6% -> 0% of each run, Pallas kernels for 0% -> 0%
where the time goes in v1:
time: 125 us
  blocking collectives  64.9 us (52%)
  waiting for transfers between devices  28.2 us (23%)
  Pallas kernels  13.6 us (11%)
  starting transfers between devices  10.4 us (8%)
  other arithmetic  4.55 us (4%)
  local copies, waits for them, and re-layouts  2.57 us (2%)
    all_gather x1, blocking collectives, body(): lax.all_gather(flat_flows, ('gz', 'row', 'col'), axis=0, tiled=True)  64.9 us
    pallas_call x1, Pallas kernels, body(): pl.pallas_call(kernel, out_shape=jax.ShapeDtypeStruct((8, LAGS), jnp.floa...  13.6 us
    ppermute x1, waiting for transfers between devices, shifted(): return lax.ppermute(value, axis, pairs)  11.8 us
    ppermute x2, waiting for transfers between devices, with_halo(): after = lax.ppermute(first, axis, down)  8.89 us
    ppermute x2, waiting for transfers between devices, with_halo(): before = lax.ppermute(last, axis, up)  7.48 us
    ppermute x2, starting transfers between devices, with_halo(): before = lax.ppermute(last, axis, up)  4.82 us
    concatenate x1, other arithmetic, with_halo(): shard = jnp.concatenate([before, shard, after], axis=dim)  3.3 us
    ppermute x1, starting transfers between devices, shifted(): return lax.ppermute(value, axis, pairs)  3.03 us
  transfers between devices with their start and end apart: 5, of which 4 were waited for; matrix products, arithmetic and copies ran while one was open for 0% of the time, Pallas kernels for 0%

profile of v1, /device:TPU:0, one launch (start us, length us, event | category | flops | bytes accessed | tf_op | source)
XLA Modules:
  0.0 125.2 jit_solution(9454575257697771597)
XLA Ops:
  0.0 0.0 copy-start.5
  0.0 1.2 slice.18
  1.2 3.0 %collective-permute-start = (bf16[1,512,512]{2,1,0:T(8,128)(2,1)S(1)}, bf16[1,512,512]{2,1,0:T(8,128)(2,1)S(1)}, u32[]{:S(2)}, u32[]{:S(2)}) collective-permute-start(bf16[1,512,512]{2,1,0:T(8,128)(2,1)S(1)} %slice.18), channel_id=1, source_target_pairs={{0,16},{16,0},{1,17},{17,1},{2,18},{18,2},{3,19},{19,3},{4,20},{20... | collective-permute-start | bytes 1572872 | tf_op jit(solution)/shard_map/ppermute | solution.py:162
  4.2 0.0 copy-done.5
  4.2 0.1 constant_dynamic-update-slice_fusion.1
  4.3 11.8 %collective-permute-done = bf16[1,512,512]{2,1,0:T(8,128)(2,1)S(1)} collective-permute-done((bf16[1,512,512]{2,1,0:T(8,128)(2,1)S(1)}, bf16[1,512,512]{2,1,0:T(8,128)(2,1)S(1)}, u32[]{:S(2)}, u32[]{:S(2)}) %collective-permute-start) | collective-permute-done | bytes 524320 | tf_op jit(solution)/shard_map/ppermute | solution.py:162
  16.2 0.1 fusion.4
  16.2 1.3 %collective-permute-start.1 = (bf16[3,128,512]{2,1,0:T(8,128)(2,1)S(1)}, bf16[3,128,512]{2,1,0:T(8,128)(2,1)S(1)}, u32[]{:S(2)}, u32[]{:S(2)}) collective-permute-start(bf16[3,128,512]{2,1,0:T(8,128)(2,1)S(1)} %get-tuple-element.7), channel_id=1, source_target_pairs={{0,4},{4,8},{8,12},{1,5},{5,9},{9,13},{2,6},{6,10},{10,14},{3,7},{... | collective-permute-start | bytes 1179656 | tf_op jit(solution)/shard_map/ppermute | solution.py:153
  17.5 0.0 copy-start.6
  17.6 0.0 copy-start.7
  17.6 1.3 %collective-permute-start.2 = (bf16[3,128,512]{2,1,0:T(8,128)(2,1)S(1)}, bf16[3,128,512]{2,1,0:T(8,128)(2,1)S(1)}, u32[]{:S(2)}, u32[]{:S(2)}) collective-permute-start(bf16[3,128,512]{2,1,0:T(8,128)(2,1)S(1)} %get-tuple-element.8), channel_id=1, source_target_pairs={{4,0},{8,4},{12,8},{5,1},{9,5},{13,9},{6,2},{10,6},{14,10},{7,3},{... | collective-permute-start | bytes 1179656 | tf_op jit(solution)/shard_map/ppermute | solution.py:154
  18.9 0.0 collective-permute-done.1
  18.9 4.3 %collective-permute-done.2 = bf16[3,128,512]{2,1,0:T(8,128)(2,1)S(1)} collective-permute-done((bf16[3,128,512]{2,1,0:T(8,128)(2,1)S(1)}, bf16[3,128,512]{2,1,0:T(8,128)(2,1)S(1)}, u32[]{:S(2)}, u32[]{:S(2)}) %collective-permute-start.2) | collective-permute-done | bytes 393248 | tf_op jit(solution)/shard_map/ppermute | solution.py:154
  23.2 1.2 pad_maximum_fusion.3
  24.4 3.5 %collective-permute-start.3 = (bf16[3,768,128]{2,1,0:T(8,128)(2,1)}, bf16[3,768,128]{2,1,0:T(8,128)(2,1)S(1)}, u32[]{:S(2)}, u32[]{:S(2)}) collective-permute-start(bf16[3,768,128]{2,1,0:T(8,128)(2,1)} %get-tuple-element.5), channel_id=1, source_target_pairs={{0,1},{1,2},{2,3},{4,5},{5,6},{6,7},{8,9},{9,10},{10,11},{12,13},{... | collective-permute-start | bytes 1769480 | tf_op jit(solution)/shard_map/ppermute | solution.py:153
  27.9 1.3 %collective-permute-start.4 = (bf16[3,768,128]{2,1,0:T(8,128)(2,1)}, bf16[3,768,128]{2,1,0:T(8,128)(2,1)S(1)}, u32[]{:S(2)}, u32[]{:S(2)}) collective-permute-start(bf16[3,768,128]{2,1,0:T(8,128)(2,1)} %get-tuple-element.6), channel_id=1, source_target_pairs={{1,0},{2,1},{3,2},{5,4},{6,5},{7,6},{9,8},{10,9},{11,10},{13,12},{... | collective-permute-start | bytes 1769480 | tf_op jit(solution)/shard_map/ppermute | solution.py:154
  29.2 0.0 copy-done.6
  29.2 0.1 reshape.15.pri_ref
  29.3 0.0 copy-done.7
  29.3 0.1 dynamic_slice.3
  29.4 0.0 copy-start
  29.4 0.0 copy-start.1
  29.4 0.0 copy-start.2
  29.4 0.0 copy-start.3
  29.4 0.0 copy-start.4
  29.4 7.5 %collective-permute-done.3 = bf16[3,768,128]{2,1,0:T(8,128)(2,1)S(1)} collective-permute-done((bf16[3,768,128]{2,1,0:T(8,128)(2,1)}, bf16[3,768,128]{2,1,0:T(8,128)(2,1)S(1)}, u32[]{:S(2)}, u32[]{:S(2)}) %collective-permute-start.3) | collective-permute-done | bytes 589856 | tf_op jit(solution)/shard_map/ppermute | solution.py:153
  36.9 4.6 %collective-permute-done.4 = bf16[3,768,128]{2,1,0:T(8,128)(2,1)S(1)} collective-permute-done((bf16[3,768,128]{2,1,0:T(8,128)(2,1)}, bf16[3,768,128]{2,1,0:T(8,128)(2,1)S(1)}, u32[]{:S(2)}, u32[]{:S(2)}) %collective-permute-start.4) | collective-permute-done | bytes 589856 | tf_op jit(solution)/shard_map/ppermute | solution.py:154
  41.5 3.3 %pad_maximum_fusion.ext = bf16[3,768,768]{2,1,0:T(8,128)(2,1)} fusion(bf16[3,768,128]{2,1,0:T(8,128)(2,1)S(1)} %collective-permute-done.4, bf16[3,128,512]{2,1,0:T(8,128)(2,1)S(1)} %collective-permute-done.2, bf16[3,512,512]{2,1,0:T(8,128)(2,1)S(1)} %constant_dynamic-update-slice_fusion, bf16[3,128,512]{2,1,0:T(8,128)(2,1)S(1)} %collective-permute-done.1, ...), kind=kLoop, calls=%fused_computation | loop fusion | flops 17694720 | bytes 7077888 | tf_op jit(solution)/shard_map/concatenate | solution.py:155
  44.8 0.0 copy-done
  44.8 0.0 copy-done.1
  44.8 0.0 copy-done.2
  44.8 0.0 copy-done.3
  44.8 0.0 copy-done.4
  44.8 13.6 %shard_map.82 = f32[8,128]{1,0:T(8,128)S(1)} custom-call(s32[16]{0:T(128)S(1)} %reshape.15.pri_ref, bf16[3,768,768]{2,1,0:T(8,128)(2,1)} %pad_maximum_fusion.ext, bf16[544,512]{1,0:T(8,128)(2,1)S(1)} %copy-done.1, bf16[4,256,256]{2,1,0:T(8,128)(2,1)S(1)} %copy-done.2, f32[4,256,128]{2,1,0:T(8,128)S(1)} %copy-done.3, f32[4,256,128]{2,1,0:T(8,128)S(1)} %copy-done.4, ...), custom_call_target="tpu_custom_call" | custom-call | tf_op jit(solution)/shard_map/pallas_call | solution.py:175
  58.4 0.1 copy.14
  58.5 0.1 reshape.19
  58.6 64.9 %all-gather = f32[32,1,16]{2,1,0:T(1,128)S(1)} all-gather(f32[1,1,16]{2,1,0:T(1,128)S(1)} %reshape.19), channel_id=1, replica_groups=mesh['gz'=2,'row'=4,'col'=4] {'gz','row','col'}, dimensions={0}, use_global_device_ids=true | all-gather | bytes 2112 | tf_op jit(solution)/shard_map/all_gather | solution.py:195
  123.6 0.1 copy.15
  123.6 0.1 reshape.17
  123.7 0.5 copy.16
  124.2 0.1 reshape.18
  124.4 0.1 dot_general.8
  124.5 0.8 fusion
  (3 shorter events, 0.0 us)
Async XLA Ops:
  0.0 4.2 %copy-start.5 = (bf16[2,512,512]{2,1,0:T(8,128)(2,1)S(1)}, bf16[2,512,512]{2,1,0:T(8,128)(2,1)}, u32[]{:S(2)}) copy-start(bf16[2,512,512]{2,1,0:T(8,128)(2,1)} %param.8) | copy-start | bytes 3145732
  1.2 15.0 %collective-permute-start = (bf16[1,512,512]{2,1,0:T(8,128)(2,1)S(1)}, bf16[1,512,512]{2,1,0:T(8,128)(2,1)S(1)}, u32[]{:S(2)}, u32[]{:S(2)}) collective-permute-start(bf16[1,512,512]{2,1,0:T(8,128)(2,1)S(1)} %slice.18), channel_id=1, source_target_pairs={{0,16},{16,0},{1,17},{17,1},{2,18},{18,2},{3,19},{19,3},{4,20},{20... | collective-permute-start | bytes 1572872 | tf_op jit(solution)/shard_map/ppermute | solution.py:162
  16.2 2.6 %collective-permute-start.1 = (bf16[3,128,512]{2,1,0:T(8,128)(2,1)S(1)}, bf16[3,128,512]{2,1,0:T(8,128)(2,1)S(1)}, u32[]{:S(2)}, u32[]{:S(2)}) collective-permute-start(bf16[3,128,512]{2,1,0:T(8,128)(2,1)S(1)} %get-tuple-element.7), channel_id=1, source_target_pairs={{0,4},{4,8},{8,12},{1,5},{5,9},{9,13},{2,6},{6,10},{10,14},{3,7},{... | collective-permute-start | bytes 1179656 | tf_op jit(solution)/shard_map/ppermute | solution.py:153
  17.5 11.7 %copy-start.6 = (s32[2,2,2,2]{3,2,1,0:T(2,128)S(1)}, s32[2,2,2,2]{3,2,1,0:T(2,128)}, u32[]{:S(2)}) copy-start(s32[2,2,2,2]{3,2,1,0:T(2,128)} %param.9) | copy-start | bytes 196
  17.6 11.8 %copy-start.7 = (s32[8]{0:T(128)S(1)}, s32[8]{0:T(128)}, u32[]{:S(2)}) copy-start(s32[8]{0:T(128)} %param.10) | copy-start | bytes 100
  17.6 5.6 %collective-permute-start.2 = (bf16[3,128,512]{2,1,0:T(8,128)(2,1)S(1)}, bf16[3,128,512]{2,1,0:T(8,128)(2,1)S(1)}, u32[]{:S(2)}, u32[]{:S(2)}) collective-permute-start(bf16[3,128,512]{2,1,0:T(8,128)(2,1)S(1)} %get-tuple-element.8), channel_id=1, source_target_pairs={{4,0},{8,4},{12,8},{5,1},{9,5},{13,9},{6,2},{10,6},{14,10},{7,3},{... | collective-permute-start | bytes 1179656 | tf_op jit(solution)/shard_map/ppermute | solution.py:154
  24.4 12.5 %collective-permute-start.3 = (bf16[3,768,128]{2,1,0:T(8,128)(2,1)}, bf16[3,768,128]{2,1,0:T(8,128)(2,1)S(1)}, u32[]{:S(2)}, u32[]{:S(2)}) collective-permute-start(bf16[3,768,128]{2,1,0:T(8,128)(2,1)} %get-tuple-element.5), channel_id=1, source_target_pairs={{0,1},{1,2},{2,3},{4,5},{5,6},{6,7},{8,9},{9,10},{10,11},{12,13},{... | collective-permute-start | bytes 1769480 | tf_op jit(solution)/shard_map/ppermute | solution.py:153
  27.9 13.6 %collective-permute-start.4 = (bf16[3,768,128]{2,1,0:T(8,128)(2,1)}, bf16[3,768,128]{2,1,0:T(8,128)(2,1)S(1)}, u32[]{:S(2)}, u32[]{:S(2)}) collective-permute-start(bf16[3,768,128]{2,1,0:T(8,128)(2,1)} %get-tuple-element.6), channel_id=1, source_target_pairs={{1,0},{2,1},{3,2},{5,4},{6,5},{7,6},{9,8},{10,9},{11,10},{13,12},{... | collective-permute-start | bytes 1769480 | tf_op jit(solution)/shard_map/ppermute | solution.py:154
  29.4 15.4 %copy-start = (f32[5,256,128]{2,1,0:T(8,128)S(1)}, f32[5,256,128]{2,1,0:T(8,128)}, u32[]{:S(2)}) copy-start(f32[5,256,128]{2,1,0:T(8,128)} %constant.25.clone.row_ref) | copy-start | bytes 1966084
  29.4 15.4 %copy-start.1 = (bf16[544,512]{1,0:T(8,128)(2,1)S(1)}, bf16[544,512]{1,0:T(8,128)(2,1)}, u32[]{:S(2)}) copy-start(bf16[544,512]{1,0:T(8,128)(2,1)} %constant.21.clone.dft_ref) | copy-start | bytes 1671172
  29.4 15.4 %copy-start.2 = (bf16[4,256,256]{2,1,0:T(8,128)(2,1)S(1)}, bf16[4,256,256]{2,1,0:T(8,128)(2,1)}, u32[]{:S(2)}) copy-start(bf16[4,256,256]{2,1,0:T(8,128)(2,1)} %constant.22.clone.wg_ref) | copy-start | bytes 1572868
  29.4 15.4 %copy-start.3 = (f32[4,256,128]{2,1,0:T(8,128)S(1)}, f32[4,256,128]{2,1,0:T(8,128)}, u32[]{:S(2)}) copy-start(f32[4,256,128]{2,1,0:T(8,128)} %constant.23.clone.colc_ref) | copy-start | bytes 1572868
  29.4 15.4 %copy-start.4 = (f32[4,256,128]{2,1,0:T(8,128)S(1)}, f32[4,256,128]{2,1,0:T(8,128)}, u32[]{:S(2)}) copy-start(f32[4,256,128]{2,1,0:T(8,128)} %constant.24.clone.cols_ref) | copy-start | bytes 1572868

commit v2 on v1

--- a/solution.py
+++ b/solution.py
@@ -125,88 +125,260 @@
     return p.astype(f32) + row_m / total, q.astype(f32) + col_m / total
 
 
-def kernel(pri_ref, ext, dft_ref, wg_ref, colc_ref, cols_ref, row_ref, out_ref, spec_ref, pq_ref):
-    def spectra(n, carry):
-        spectrum_pair(ext, n // 2, n % 2, dft_ref, wg_ref, spec_ref, pq_ref, n * 2)
-        return carry
-
-    lax.fori_loop(0, 6, spectra, 0)
-    lane = lax.broadcasted_iota(jnp.int32, (1, LAGS), 1)
-
-    def pairs(n, carry):
-        a, b = pair_flow(
-            n, n + 4, pri_ref[n], pri_ref[8 + n], spec_ref, colc_ref, cols_ref, row_ref
+def make_kernel(sizes, rows_each):
+    size_gz, size_row, size_col = sizes
+    count = size_gz * size_row * size_col
+    side = 2 * STRIDE
+    margin = HALO // 2
+    far = side - margin
+    mesh_id = pl.DeviceIdType.MESH
+    steps = [(a, b) for a in (-1, 0, 1) for b in (-1, 0, 1) if (a, b) != (0, 0)]
+    halo_span = {-1: (0, margin), 0: (margin, side), 1: (margin + side, margin)}
+    edge_span = {-1: (0, margin), 0: (0, side), 1: (far, margin)}
+    chunks = (
+        (0, side, 0, margin),
+        (0, side, far, margin),
+        (0, margin, margin, far - margin),
+        (far, margin, margin, far - margin),
+        (margin, far - margin, margin, far - margin),
+    )
+    needs = {(0, -1): 1, (-1, -1): 1, (1, -1): 1, (0, 1): 2, (-1, 1): 2, (1, 1): 2, (-1, 0): 3}
+    needs[(1, 0)] = 4
+
+    def kernel(
+        pri_ref, order_ref, sec_hbm, dft_hbm, wg_hbm, colc_hbm, cols_hbm, row_hbm, out_ref,
+        ext, dft_ref, wg_ref, colc_ref, cols_ref, row_ref, spec_ref, pq_ref, mine_ref, all_ref,
+        load_sem, own_send, own_recv, next_send, next_recv, chunk_send, chunk_recv, flow_send,
+        flow_recv,
+    ):
+        gz, row, col = lax.axis_index("gz"), lax.axis_index("row"), lax.axis_index("col")
+        flat = (gz * size_row + row) * size_col + col
+
+        def device(number):
+            return (
+                number // (size_row * size_col),
+                (number // size_col) % size_row,
+                number % size_col,
+            )
+
+        loads = [
+            pltpu.make_async_copy(
+                sec_hbm, ext.at[0:2, margin : margin + side, margin : margin + side],
+                load_sem.at[0],
+            )
+        ]
+        tables = (
+            (dft_hbm, dft_ref), (wg_hbm, wg_ref), (colc_hbm, colc_ref), (cols_hbm, cols_ref),
+            (row_hbm, row_ref),
         )
-        out_ref[pl.ds(n, 1), :] = jnp.where(lane == 0, a, b)
-        return carry
-
-    lax.fori_loop(0, 8, pairs, 0)
-
-
-def with_halo(shard, sides, width):
-    for axis, dim in sides:
-        devices, length = (lax.axis_size(axis), shard.shape[dim])
-        up = [(i, (i + 1) % devices) for i in range(devices - 1)]
-        down = [(j, i) for i, j in up]
-        last = lax.slice_in_dim(shard, length - width, length, axis=dim)
-        first = lax.slice_in_dim(shard, 0, width, axis=dim)
-        before = lax.ppermute(last, axis, up)
-        after = lax.ppermute(first, axis, down)
-        shard = jnp.concatenate([before, shard, after], axis=dim)
-    return shard
-
-
-def shifted(value, axis, steps):
-    count = lax.axis_size(axis)
-    pairs = [(source, (source + steps) % count) for source in range(count)]
-    return lax.ppermute(value, axis, pairs)
+        for n, (source, target) in enumerate(tables):
+            loads.append(pltpu.make_async_copy(source, target, load_sem.at[n + 1]))
+        for copy in loads:
+            copy.start()
+
+        barrier = pltpu.get_barrier_semaphore()
+
+        def greet(n, carry):
+            other = (flat + n) % count
+            pl.semaphore_signal(barrier, 1, device_id=device(other), device_id_type=mesh_id)
+            return carry
+
+        lax.fori_loop(1, count, greet, 0)
+
+        def exists(step):
+            a, b = step
+            ok = None
+            for delta, place, size in ((a, row, size_row), (b, col, size_col)):
+                if delta:
+                    this = place > 0 if delta < 0 else place < size - 1
+                    ok = this if ok is None else jnp.logical_and(ok, this)
+            return ok
+
+        def region(step):
+            (r0, rn), (c0, cn) = halo_span[step[0]], halo_span[step[1]]
+            return slice(r0, r0 + rn), slice(c0, c0 + cn)
+
+        def edge(step, offset):
+            (r0, rn), (c0, cn) = edge_span[step[0]], edge_span[step[1]]
+            return slice(r0 + offset, r0 + rn + offset), slice(c0 + offset, c0 + cn + offset)
+
+        def own_copy(n):
+            step = steps[n]
+            back = (-step[0], -step[1])
+            return pltpu.make_async_remote_copy(
+                src_ref=sec_hbm.at[(slice(0, 2), *edge(step, 0))],
+                dst_ref=ext.at[(slice(0, 2), *region(back))],
+                send_sem=own_send.at[n], recv_sem=own_recv.at[steps.index(back)],
+                device_id=(gz, row + step[0], col + step[1]), device_id_type=mesh_id,
+            )
+
+        def next_copy(n):
+            step = steps[n]
+            back = (-step[0], -step[1])
+            return pltpu.make_async_remote_copy(
+                src_ref=ext.at[(2, *edge(step, margin))],
+                dst_ref=ext.at[(2, *region(back))],
+                send_sem=next_send.at[n], recv_sem=next_recv.at[steps.index(back)],
+                device_id=(gz, row + step[0], col + step[1]), device_id_type=mesh_id,
+            )
+
+        def own_wait(n):
+            ref = ext.at[(slice(0, 2), *region(steps[n]))]
+            pltpu.make_async_copy(ref, ref, own_recv.at[n]).wait()
+
+        def next_wait(n):
+            ref = ext.at[(2, *region(steps[n]))]
+            pltpu.make_async_copy(ref, ref, next_recv.at[n]).wait()
+
+        def chunk_copy(n):
+            r0, rn, c0, cn = chunks[n]
+            return pltpu.make_async_remote_copy(
+                src_ref=sec_hbm.at[0, r0 : r0 + rn, c0 : c0 + cn],
+                dst_ref=ext.at[
+                    2, margin + r0 : margin + r0 + rn, margin + c0 : margin + c0 + cn
+                ],
+                send_sem=chunk_send.at[n], recv_sem=chunk_recv.at[n],
+                device_id=((gz + size_gz - 1) % size_gz, row, col), device_id_type=mesh_id,
+            )
+
+        for n, step in enumerate(steps):
+            @pl.when(jnp.logical_not(exists(step)))
+            def _(step=step):
+                rows, cols = region(step)
+                ext[:, rows, cols] = jnp.zeros(
+                    (3, rows.stop - rows.start, cols.stop - cols.start), ext.dtype
+                )
+
+        mine_ref[...] = jnp.zeros_like(mine_ref)
+        pl.semaphore_wait(barrier, count - 1)
+        for n in range(len(chunks)):
+            chunk_copy(n).start()
+        for n, step in enumerate(steps):
+            @pl.when(exists(step))
+            def _(n=n):
+                own_copy(n).start()
+        for copy in loads:
+            copy.wait()
+        for n, step in enumerate(steps):
+            @pl.when(exists(step))
+            def _(n=n):
+                own_wait(n)
+
+        def spectra(n, carry):
+            spectrum_pair(ext, n // 2, n % 2, dft_ref, wg_ref, spec_ref, pq_ref, n * 2)
+            return carry
+
+        def forward(low, high):
+            for n in range(low, high):
+                chunk_copy(n).wait_recv()
+                for m, step in enumerate(steps):
+                    if needs[step] == n + 1:
+                        @pl.when(exists(step))
+                        def _(m=m):
+                            next_copy(m).start()
+
+        lane = lax.broadcasted_iota(jnp.int32, (1, LAGS), 1)
+        sections, columns = 2 * size_gz, 2 * size_col
+
+        def pairs(n, carry):
+            a, b = pair_flow(
+                n, n + 4, pri_ref[n], pri_ref[8 + n], spec_ref, colc_ref, cols_ref, row_ref
+            )
+            i = (n // 2) % 2
+            at = (2 * gz + n // 4) * columns + 2 * col + n % 2
+            mine_ref[i] = (
+                mine_ref[i]
+                + jnp.where(lane == at, a, 0.0)
+                + jnp.where(lane == at + sections * columns, b, 0.0)
+            )
+            return carry
+
+        lax.fori_loop(0, 4, spectra, 0)
+        forward(0, 2)
+        lax.fori_loop(0, 4, pairs, 0)
+        forward(2, 5)
+        for n, step in enumerate(steps):
+            @pl.when(exists(step))
+            def _(n=n):
+                next_wait(n)
+        lax.fori_loop(4, 6, spectra, 0)
+        lax.fori_loop(4, 8, pairs, 0)
+
+        total_rows = 2 * size_row
+        slot = gz * size_col + col
+        place = slot * total_rows + 2 * row
+
+        def flow_copy(n):
+            return pltpu.make_async_remote_copy(
+                src_ref=mine_ref, dst_ref=all_ref.at[pl.ds(place, 2)],
+                send_sem=flow_send, recv_sem=flow_recv,
+                device_id=device((flat + n) % count), device_id_type=mesh_id,
+            )
+
+        def send(n, carry):
+            flow_copy(n).start()
+            return carry
+
+        lax.fori_loop(1, count, send, 0)
+        all_ref[place] = mine_ref[0]
+        all_ref[place + 1] = mine_ref[1]
+        for n in range(len(chunks)):
+            chunk_copy(n).wait_send()
+        for n, step in enumerate(steps):
+            @pl.when(exists(step))
+            def _(n=n):
+                own_copy(n).wait_send()
+                next_copy(n).wait_send()
+        got = all_ref.at[pl.ds(0, 2 * (count - 1))]
+        pltpu.make_async_copy(got, got, flow_recv).wait()
+        for m in range(rows_each):
+            wanted = order_ref[row * rows_each + m]
+            value = all_ref[wanted]
+            for other in range(1, size_gz * size_col):
+                value = value + all_ref[other * total_rows + wanted]
+            out_ref[m : m + 1, :] = value
+        pltpu.make_async_copy(got, got, flow_send).wait()
+
+    return kernel
 
 
 def body(sections, priors, row_order):
-    sec_count = sections.shape[0]
-    per_side = sections.shape[1] // STRIDE
-    place_count = per_side * per_side
-    arrived = shifted(sections[:1], "gz", -1)
-    extended = with_halo(
-        jnp.concatenate([sections, arrived], axis=0), (("row", 1), ("col", 2)), HALO // 2
-    )
+    sizes = tuple(lax.axis_size(name) for name in ("gz", "row", "col"))
+    count = math.prod(sizes)
+    rows_each = row_order.shape[0] // sizes[1]
+    width = 2 * 2 * sizes[0] * 2 * sizes[2]
     colc, cols, row = lag_tables()
-    vmem = pl.BlockSpec(memory_space=pltpu.VMEM)
-    flows = pl.pallas_call(
-        kernel,
-        out_shape=jax.ShapeDtypeStruct((8, LAGS), jnp.float32),
-        in_specs=[pl.BlockSpec(memory_space=pltpu.SMEM)] + [vmem] * 6,
-        out_specs=vmem,
-        scratch_shapes=[
-            pltpu.VMEM((12, KROWS, 2 * PATCH), jnp.bfloat16),
-            pltpu.VMEM((2 * KROWS, 768), jnp.float32),
-        ],
-        compiler_params=pltpu.CompilerParams(vmem_limit_bytes=50 << 20),
-    )(
-        priors.reshape(-1),
-        extended,
+    tables = (
         bf16_const(dft_table()),
         bf16_const(split_tables()),
         f32_const(lane_tiles(colc)),
         f32_const(lane_tiles(cols)),
         f32_const(lane_tiles(row)),
     )
-    flat_flows = flows[:, :2].T.reshape(1, 2 * sec_count * place_count)
-    gathered = lax.all_gather(flat_flows, ("gz", "row", "col"), axis=0, tiled=True)
-    size_gz = lax.axis_size("gz")
-    size_row = lax.axis_size("row")
-    size_col = lax.axis_size("col")
-    whole_grid = gathered.reshape(size_gz, size_row, size_col, 2, sec_count, per_side, per_side)
-    whole_grid = jnp.transpose(whole_grid, (3, 0, 4, 1, 5, 2, 6)).reshape(
-        2, size_gz * sec_count, size_row * per_side, size_col * per_side
-    )
-    rows_each = row_order.shape[0] // size_row
-    owned = lax.dynamic_slice_in_dim(row_order, lax.axis_index("row") * rows_each, rows_each)
-    selector = (owned[:, None] == jnp.arange(row_order.shape[0], dtype=jnp.int32)[None, :]).astype(
-        jnp.float32
-    )
-    picked = jnp.einsum("jr,csrk->jcsk", selector, whole_grid, precision=lax.Precision.HIGHEST)
-    return picked.reshape(rows_each, 2 * size_gz * sec_count * size_col * per_side)
+    smem = pl.BlockSpec(memory_space=pltpu.SMEM)
+    hbm = pl.BlockSpec(memory_space=pl.ANY)
+    dma = pltpu.SemaphoreType.DMA
+    wide = 2 * STRIDE + HALO
+    flows = pl.pallas_call(
+        make_kernel(sizes, rows_each),
+        out_shape=jax.ShapeDtypeStruct((rows_each, LAGS), jnp.float32),
+        in_specs=[smem, smem] + [hbm] * 6,
+        out_specs=pl.BlockSpec(memory_space=pltpu.VMEM),
+        scratch_shapes=[
+            pltpu.VMEM((3, wide, wide), jnp.bfloat16),
+            *[pltpu.VMEM(t.shape, t.dtype) for t in tables],
+            pltpu.VMEM((12, KROWS, 2 * PATCH), jnp.bfloat16),
+            pltpu.VMEM((2 * KROWS, wide), jnp.float32),
+            pltpu.VMEM((2, 1, LAGS), jnp.float32),
+            pltpu.VMEM((2 * count, 1, LAGS), jnp.float32),
+            dma((6,)), dma((8,)), dma((8,)), dma((8,)), dma((8,)), dma((5,)), dma((5,)),
+            dma(()), dma(()),
+        ],
+        compiler_params=pltpu.CompilerParams(
+            vmem_limit_bytes=50 << 20, collective_id=0, has_side_effects=True
+        ),
+    )(priors.reshape(-1), row_order, sections, *tables)
+    return flows[:, :width]
 
 
 def solution(mesh):

time: 125 us -> 46.2 us (0.37)
  blocking collectives: 64.9 us -> 0 us
  waiting for transfers between devices: 28.2 us -> 0 us
  Pallas kernels: 13.6 us -> 37.9 us
  starting transfers between devices: 10.4 us -> 0 us
  local copies, waits for them, and re-layouts: 2.57 us -> 7.83 us
  other arithmetic: 4.55 us -> 0 us
    all_gather x1 -> x0, blocking collectives: 64.9 us -> none  [body(): lax.all_gather(flat_flows, ('gz', 'row', 'col'), axis=0, tiled=True)]
    ppermute x5 -> x0, waiting for transfers between devices: 28.2 us -> none  [the longest x1 11.8 us: shifted(): return lax.ppermute(value, axis, pairs)]
    pallas_call x1, Pallas kernels: 13.6 us -> 37.9 us  [body(): pl.pallas_call(make_kernel(sizes, rows_each), out_shape=jax.ShapeDtypeStr...]
    ppermute x5 -> x0, starting transfers between devices: 10.4 us -> none  [the longest x2 4.82 us: with_halo(): before = lax.ppermute(last, axis, up)]
    unnamed x18 -> x15, local copies, waits for them, and re-layouts: 0.19 us -> 7.05 us
    concatenate x1 -> x0, other arithmetic: 3.3 us -> none  [with_halo(): shard = jnp.concatenate([before, shard, after], axis=dim)]
  transfers between devices with their start and end apart: 5 -> 0, of which waited for: 4 -> 0; matrix products, arithmetic and copies ran while one was open for 0% -> 0% of each run, Pallas kernels for 0% -> 0%
where the time goes in v2:
time: 46.2 us; the launch traced here: 45.8 us
  Pallas kernels  37.9 us (82%)
  local copies, waits for them, and re-layouts  7.83 us (17%)
    pallas_call x1, Pallas kernels, body(): pl.pallas_call(make_kernel(sizes, rows_each), out_shape=jax.ShapeDtypeStr...  37.9 us
    unnamed x15, local copies, waits for them, and re-layouts  7.05 us

profile of v2, /device:TPU:0, one launch (start us, length us, event | category | flops | bytes accessed | tf_op | source)
XLA Modules:
  0.0 45.8 jit_solution(6320863168767805168)
XLA Ops:
  0.0 0.0 copy-start.6
  0.0 0.8 %reshape.3.pri_ref = s32[16]{0:T(128)S(1)} reshape(s32[2,2,2,2]{3,2,1,0:T(2,128)} %param.9) | data formatting | bytes 128 | tf_op jit(solution)/shard_map/reshape | solution.py:380
  0.8 0.0 copy-done.6
  0.8 0.0 copy-start
  0.8 1.2 %copy-done = bf16[2,512,512]{2,1,0:T(8,128)(2,1)S(1)} copy-done((bf16[2,512,512]{2,1,0:T(8,128)(2,1)S(1)}, bf16[2,512,512]{2,1,0:T(8,128)(2,1)}, u32[]{:S(2)}) %copy-start) | copy-done | bytes 1048600
  2.0 0.0 copy-start.1
  2.0 1.1 %copy-done.1 = f32[5,256,128]{2,1,0:T(8,128)S(1)} copy-done((f32[5,256,128]{2,1,0:T(8,128)S(1)}, f32[5,256,128]{2,1,0:T(8,128)}, u32[]{:S(2)}) %copy-start.1) | copy-done | bytes 655384
  3.1 0.0 copy-start.2
  3.1 1.1 %copy-done.2 = bf16[544,512]{1,0:T(8,128)(2,1)S(1)} copy-done((bf16[544,512]{1,0:T(8,128)(2,1)S(1)}, bf16[544,512]{1,0:T(8,128)(2,1)}, u32[]{:S(2)}) %copy-start.2) | copy-done | bytes 557080
  4.2 0.0 copy-start.3
  4.2 1.0 %copy-done.3 = f32[4,256,128]{2,1,0:T(8,128)S(1)} copy-done((f32[4,256,128]{2,1,0:T(8,128)S(1)}, f32[4,256,128]{2,1,0:T(8,128)}, u32[]{:S(2)}) %copy-start.3) | copy-done | bytes 524312
  5.2 0.0 copy-start.4
  5.2 1.0 %copy-done.4 = f32[4,256,128]{2,1,0:T(8,128)S(1)} copy-done((f32[4,256,128]{2,1,0:T(8,128)S(1)}, f32[4,256,128]{2,1,0:T(8,128)}, u32[]{:S(2)}) %copy-start.4) | copy-done | bytes 524312
  6.2 0.0 copy-start.5
  6.2 1.0 %copy-done.5 = bf16[4,256,256]{2,1,0:T(8,128)(2,1)S(1)} copy-done((bf16[4,256,256]{2,1,0:T(8,128)(2,1)S(1)}, bf16[4,256,256]{2,1,0:T(8,128)(2,1)}, u32[]{:S(2)}) %copy-start.5) | copy-done | bytes 524312
  7.3 37.9 %shard_map.82 = f32[2,128]{1,0:T(2,128)S(1)} custom-call(s32[16]{0:T(128)S(1)} %reshape.3.pri_ref, s32[8]{0:T(128)S(1)} %copy-done.6, bf16[2,512,512]{2,1,0:T(8,128)(2,1)S(1)} %copy-done, bf16[544,512]{1,0:T(8,128)(2,1)S(1)} %copy-done.2, bf16[4,256,256]{2,1,0:T(8,128)(2,1)S(1)} %copy-done.5, f32[4,256,128]{2,1,0:T(8,128)S(1)} %copy-done.4, ...), custom_call_target="tpu_custom_call" | custom-call | tf_op jit(solution)/shard_map/pallas_call | solution.py:362
  45.2 0.6 %copy.10 = f32[2,64]{1,0:T(2,128)} copy(f32[2,64]{1,0:T(2,128)S(1)} %bitcast.1) | data formatting | bytes 1024
Async XLA Ops:
  0.0 0.8 %copy-start.6 = (s32[8]{0:T(128)S(1)}, s32[8]{0:T(128)}, u32[]{:S(2)}) copy-start(s32[8]{0:T(128)} %order_ref.1) | copy-start | bytes 100
  0.8 1.2 %copy-start = (bf16[2,512,512]{2,1,0:T(8,128)(2,1)S(1)}, bf16[2,512,512]{2,1,0:T(8,128)(2,1)}, u32[]{:S(2)}) copy-start(bf16[2,512,512]{2,1,0:T(8,128)(2,1)} %sec_hbm.1) | copy-start | bytes 3145732
  2.0 1.1 %copy-start.1 = (f32[5,256,128]{2,1,0:T(8,128)S(1)}, f32[5,256,128]{2,1,0:T(8,128)}, u32[]{:S(2)}) copy-start(f32[5,256,128]{2,1,0:T(8,128)} %constant.14.clone.row_hbm) | copy-start | bytes 1966084
  3.1 1.1 %copy-start.2 = (bf16[544,512]{1,0:T(8,128)(2,1)S(1)}, bf16[544,512]{1,0:T(8,128)(2,1)}, u32[]{:S(2)}) copy-start(bf16[544,512]{1,0:T(8,128)(2,1)} %constant.10.clone.dft_hbm) | copy-start | bytes 1671172
  4.2 1.0 %copy-start.3 = (f32[4,256,128]{2,1,0:T(8,128)S(1)}, f32[4,256,128]{2,1,0:T(8,128)}, u32[]{:S(2)}) copy-start(f32[4,256,128]{2,1,0:T(8,128)} %constant.13.clone.cols_hbm) | copy-start | bytes 1572868
  5.2 1.0 %copy-start.4 = (f32[4,256,128]{2,1,0:T(8,128)S(1)}, f32[4,256,128]{2,1,0:T(8,128)}, u32[]{:S(2)}) copy-start(f32[4,256,128]{2,1,0:T(8,128)} %constant.12.clone.colc_hbm) | copy-start | bytes 1572868
  6.2 1.0 %copy-start.5 = (bf16[4,256,256]{2,1,0:T(8,128)(2,1)S(1)}, bf16[4,256,256]{2,1,0:T(8,128)(2,1)}, u32[]{:S(2)}) copy-start(bf16[4,256,256]{2,1,0:T(8,128)(2,1)} %constant.11.clone.wg_hbm) | copy-start | bytes 1572868

commit v3 on v2

--- a/solution.py
+++ b/solution.py
@@ -280,29 +280,33 @@
         lane = lax.broadcasted_iota(jnp.int32, (1, LAGS), 1)
         sections, columns = 2 * size_gz, 2 * size_col
 
-        def pairs(n, carry):
-            a, b = pair_flow(
-                n, n + 4, pri_ref[n], pri_ref[8 + n], spec_ref, colc_ref, cols_ref, row_ref
-            )
-            i = (n // 2) % 2
-            at = (2 * gz + n // 4) * columns + 2 * col + n % 2
-            mine_ref[i] = (
-                mine_ref[i]
-                + jnp.where(lane == at, a, 0.0)
-                + jnp.where(lane == at + sections * columns, b, 0.0)
-            )
-            return carry
-
-        lax.fori_loop(0, 4, spectra, 0)
+        def prior(part, n):
+            return pri_ref[part, n // 4, (n // 2) % 2, n % 2]
+
+        def pairs_static(low, high):
+            values = []
+            for n in range(low, high):
+                a, b = pair_flow(
+                    n, n + 4, prior(0, n), prior(1, n), spec_ref, colc_ref, cols_ref, row_ref
+                )
+                at = (2 * gz + n // 4) * columns + 2 * col + n % 2
+                values.append(
+                    jnp.where(lane == at, a, 0.0)
+                    + jnp.where(lane == at + sections * columns, b, 0.0)
+                )
+            mine_ref[0] = mine_ref[0] + values[0] + values[1]
+            mine_ref[1] = mine_ref[1] + values[2] + values[3]
+
+        lax.fori_loop(0, 4, spectra, 0, unroll=2)
         forward(0, 2)
-        lax.fori_loop(0, 4, pairs, 0)
+        pairs_static(0, 4)
         forward(2, 5)
         for n, step in enumerate(steps):
             @pl.when(exists(step))
             def _(n=n):
                 next_wait(n)
-        lax.fori_loop(4, 6, spectra, 0)
-        lax.fori_loop(4, 8, pairs, 0)
+        lax.fori_loop(4, 6, spectra, 0, unroll=2)
+        pairs_static(4, 8)
 
         total_rows = 2 * size_row
         slot = gz * size_col + col
@@ -336,7 +340,7 @@
             value = all_ref[wanted]
             for other in range(1, size_gz * size_col):
                 value = value + all_ref[other * total_rows + wanted]
-            out_ref[m : m + 1, :] = value
+            out_ref[m : m + 1, :] = value[:, : out_ref.shape[1]]
         pltpu.make_async_copy(got, got, flow_send).wait()
 
     return kernel
@@ -361,7 +365,7 @@
     wide = 2 * STRIDE + HALO
     flows = pl.pallas_call(
         make_kernel(sizes, rows_each),
-        out_shape=jax.ShapeDtypeStruct((rows_each, LAGS), jnp.float32),
+        out_shape=jax.ShapeDtypeStruct((rows_each, width), jnp.float32),
         in_specs=[smem, smem] + [hbm] * 6,
         out_specs=pl.BlockSpec(memory_space=pltpu.VMEM),
         scratch_shapes=[
@@ -375,10 +379,10 @@
             dma(()), dma(()),
         ],
         compiler_params=pltpu.CompilerParams(
-            vmem_limit_bytes=50 << 20, collective_id=0, has_side_effects=True
+            vmem_limit_bytes=67043328, collective_id=0, has_side_effects=True
         ),
-    )(priors.reshape(-1), row_order, sections, *tables)
-    return flows[:, :width]
+    )(priors, row_order, sections, *tables)
+    return flows
 
 
 def solution(mesh):

time: 46.2 us -> 38.6 us (0.84)
  local copies, waits for them, and re-layouts: 7.83 us -> 1.24 us
  Pallas kernels: 37.9 us -> 37.1 us
    unnamed x15 -> x1, local copies, waits for them, and re-layouts: 7.05 us -> 1.24 us
    reshape x1 -> x0, local copies, waits for them, and re-layouts: 0.78 us -> none  [body(): priors.reshape(-1)]
    pallas_call x1, Pallas kernels: 37.9 us -> 37.1 us  [body(): pl.pallas_call(make_kernel(sizes, rows_each), out_shape=jax.ShapeDtypeStr...]
where the time goes in v3:
time: 38.6 us; the launch traced here: 38.4 us
  Pallas kernels  37.1 us (96%)
  local copies, waits for them, and re-layouts  1.24 us (3%)
    pallas_call x1, Pallas kernels, body(): pl.pallas_call(make_kernel(sizes, rows_each), out_shape=jax.ShapeDtypeStr...  37.1 us
    unnamed x1, local copies, waits for them, and re-layouts  1.24 us

profile of v3, /device:TPU:0, one launch (start us, length us, event | category | flops | bytes accessed | tf_op | source)
XLA Modules:
  0.0 38.4 jit_solution(5589932066597460502)
XLA Ops:
  0.0 37.1 %shard_map.82 = f32[2,64]{1,0:T(2,128)} custom-call(s32[2,2,2,2]{3,2,1,0:T(2,128)} %pri_ref.1, s32[8]{0:T(128)} %order_ref.1, bf16[2,512,512]{2,1,0:T(8,128)(2,1)} %sec_hbm.1, bf16[544,512]{1,0:T(8,128)(2,1)} %constant.10.clone.dft_hbm, bf16[4,256,256]{2,1,0:T(8,128)(2,1)} %constant.11.clone.wg_hbm, f32[4,256,128]{2,1,0:T(8,128)} %constant.12.clone.colc_hbm, ...), custom_call_target="tpu_custom_call" | custom-call | tf_op jit(solution)/shard_map/pallas_call | solution.py:366
  37.1 1.2 %copy.10 = f32[2,64]{1,0:T(2,128)} copy(f32[2,64]{1,0:T(2,128)} %shard_map.82) | data formatting | bytes 1024

commit v4 on v3

--- a/solution.py
+++ b/solution.py
@@ -61,15 +61,27 @@
     return bf16_const(value).astype(np.float32)
 
 
-def spectrum_pair(ext, section, i, dft_ref, wg_ref, spec_ref, pq_ref, base):
-    window = ext[section, pl.ds(pl.multiple_of(i * STRIDE, STRIDE), PATCH), :]
-    pq_ref[...] = jnp.dot(dft_ref[...], window, preferred_element_type=jnp.float32)
+def first_pass(ext, section, i, dft_ref, pq_ref, slot, outer):
+    rows = pl.ds(pl.multiple_of(i * STRIDE, STRIDE), PATCH)
+    edge, far = HALO // 2, ext.shape[2] - HALO // 2
+    if not outer:
+        pq_ref[slot, :, edge:far] = jnp.dot(
+            dft_ref[...], ext[section, rows, edge:far], preferred_element_type=jnp.float32
+        )
+        return
+    window = jnp.concatenate([ext[section, rows, :edge], ext[section, rows, far:]], axis=1)
+    both = jnp.dot(dft_ref[...], window, preferred_element_type=jnp.float32)
+    pq_ref[slot, :, :edge] = both[:, :edge]
+    pq_ref[slot, :, far:] = both[:, edge:]
+
+
+def spectrum_pair(wg_ref, spec_ref, pq_ref, slot, base):
     for j in range(2):
         p, q = [], []
         for t in range(4):
             lanes = slice(j * STRIDE + t * QUARTER, j * STRIDE + (t + 1) * QUARTER)
-            p.append(pq_ref[:KROWS, lanes])
-            q.append(pq_ref[KROWS:, lanes])
+            p.append(pq_ref[slot, :KROWS, lanes])
+            q.append(pq_ref[slot, KROWS:, lanes])
         ps, pd, qs, qd = p[0] + p[2], p[0] - p[2], q[0] + q[2], q[0] - q[2]
         pt, pu, qt, qu = p[1] + p[3], p[1] - p[3], q[1] + q[3], q[1] - q[3]
         groups = ((ps + pt, qs + qt), (pd + qu, qd - pu), (ps - pt, qs - qt), (pd - qu, qd + pu))
@@ -241,6 +253,31 @@
                 device_id=((gz + size_gz - 1) % size_gz, row, col), device_id_type=mesh_id,
             )
 
+        def forward(low, high):
+            for n in range(low, high):
+                chunk_copy(n).wait_recv()
+                for m, step in enumerate(steps):
+                    if needs[step] == n + 1:
+                        @pl.when(exists(step))
+                        def _(m=m):
+                            next_copy(m).start()
+
+        def halo_waits(wait, outer):
+            for n, step in enumerate(steps):
+                if (step[1] != 0) == outer:
+                    @pl.when(exists(step))
+                    def _(n=n):
+                        wait(n)
+
+        def middle(n, carry):
+            first_pass(ext, n // 2, n % 2, dft_ref, pq_ref, n % 4, False)
+            return carry
+
+        def spectra(n, carry):
+            first_pass(ext, n // 2, n % 2, dft_ref, pq_ref, n % 4, True)
+            spectrum_pair(wg_ref, spec_ref, pq_ref, n % 4, n * 2)
+            return carry
+
         for n, step in enumerate(steps):
             @pl.when(jnp.logical_not(exists(step)))
             def _(step=step):
@@ -259,23 +296,10 @@
                 own_copy(n).start()
         for copy in loads:
             copy.wait()
-        for n, step in enumerate(steps):
-            @pl.when(exists(step))
-            def _(n=n):
-                own_wait(n)
-
-        def spectra(n, carry):
-            spectrum_pair(ext, n // 2, n % 2, dft_ref, wg_ref, spec_ref, pq_ref, n * 2)
-            return carry
-
-        def forward(low, high):
-            for n in range(low, high):
-                chunk_copy(n).wait_recv()
-                for m, step in enumerate(steps):
-                    if needs[step] == n + 1:
-                        @pl.when(exists(step))
-                        def _(m=m):
-                            next_copy(m).start()
+        halo_waits(own_wait, False)
+        lax.fori_loop(0, 4, middle, 0, unroll=2)
+        forward(0, 2)
+        halo_waits(own_wait, True)
 
         lane = lax.broadcasted_iota(jnp.int32, (1, LAGS), 1)
         sections, columns = 2 * size_gz, 2 * size_col
@@ -298,13 +322,12 @@
             mine_ref[1] = mine_ref[1] + values[2] + values[3]
 
         lax.fori_loop(0, 4, spectra, 0, unroll=2)
-        forward(0, 2)
+        forward(2, 4)
         pairs_static(0, 4)
-        forward(2, 5)
-        for n, step in enumerate(steps):
-            @pl.when(exists(step))
-            def _(n=n):
-                next_wait(n)
+        forward(4, 5)
+        halo_waits(next_wait, False)
+        lax.fori_loop(4, 6, middle, 0, unroll=2)
+        halo_waits(next_wait, True)
         lax.fori_loop(4, 6, spectra, 0, unroll=2)
         pairs_static(4, 8)
 
@@ -372,7 +395,7 @@
             pltpu.VMEM((3, wide, wide), jnp.bfloat16),
             *[pltpu.VMEM(t.shape, t.dtype) for t in tables],
             pltpu.VMEM((12, KROWS, 2 * PATCH), jnp.bfloat16),
-            pltpu.VMEM((2 * KROWS, wide), jnp.float32),
+            pltpu.VMEM((4, 2 * KROWS, wide), jnp.float32),
             pltpu.VMEM((2, 1, LAGS), jnp.float32),
             pltpu.VMEM((2 * count, 1, LAGS), jnp.float32),
             dma((6,)), dma((8,)), dma((8,)), dma((8,)), dma((8,)), dma((5,)), dma((5,)),

time: 38.6 us -> 35.1 us (0.909)
  Pallas kernels: 37.1 us -> 33.7 us
    pallas_call x1, Pallas kernels: 37.1 us -> 33.7 us  [body(): pl.pallas_call(make_kernel(sizes, rows_each), out_shape=jax.ShapeDtypeStr...]
where the time goes in v4:
time: 35.1 us; the launch traced here: 34.9 us
  Pallas kernels  33.7 us (96%)
  local copies, waits for them, and re-layouts  1.24 us (4%)
    pallas_call x1, Pallas kernels, body(): pl.pallas_call(make_kernel(sizes, rows_each), out_shape=jax.ShapeDtypeStr...  33.7 us
    unnamed x1, local copies, waits for them, and re-layouts  1.24 us

profile of v4, /device:TPU:0, one launch (start us, length us, event | category | flops | bytes accessed | tf_op | source)
XLA Modules:
  0.0 34.9 jit_solution(305105481092341007)
XLA Ops:
  0.0 33.7 %shard_map.82 = f32[2,64]{1,0:T(2,128)} custom-call(s32[2,2,2,2]{3,2,1,0:T(2,128)} %pri_ref.1, s32[8]{0:T(128)} %order_ref.1, bf16[2,512,512]{2,1,0:T(8,128)(2,1)} %sec_hbm.1, bf16[544,512]{1,0:T(8,128)(2,1)} %constant.10.clone.dft_hbm, bf16[4,256,256]{2,1,0:T(8,128)(2,1)} %constant.11.clone.wg_hbm, f32[4,256,128]{2,1,0:T(8,128)} %constant.12.clone.colc_hbm, ...), custom_call_target="tpu_custom_call" | custom-call | tf_op jit(solution)/shard_map/pallas_call | solution.py:389
  33.7 1.2 %copy.10 = f32[2,64]{1,0:T(2,128)} copy(f32[2,64]{1,0:T(2,128)} %shard_map.82) | data formatting | bytes 1024
